TPU v7x, 32 devices: a whole 2x2x4 slice. The times are simulated.
32 devices in a mesh: groups: 2 (over y), fsdp: 4 (over z), expert: 4 (over x, core).
Axes of the slice: x: 2, y: 2, z: 4, core: 2. Of those that a mesh axis runs over, the one named last changes fastest.
Arguments:
- queries: bfloat16 [512, 2048], P(('groups', 'fsdp'), 'expert'), parts along dimension 0, may hold values from -14 to 14
- keys: bfloat16 [8, 2048, 512], P(('groups', 'fsdp'), None, 'expert'), parts along dimension 0, may hold values from -14 to 14
- values: bfloat16 [8, 2048, 512], P(('groups', 'fsdp'), None, 'expert'), parts along dimension 0, may hold values from -4 to 4
- out_weight: bfloat16 [2048, 4096], P('expert', 'fsdp'), may hold values from -0.5 to 0.5
- residual: bfloat16 [512, 4096], P(('groups', 'fsdp')), parts along dimension 0, may hold values from -3 to 3
- norm_gain: float32 [4096], replicated, may hold values from 0.5 to 1.5
- route_ids: int32 [512, 2], P(('groups', 'fsdp')), parts along dimension 0, may hold values from 0 to 7, as said below
- route_slots: int32 [512, 2], P(('groups', 'fsdp')), parts along dimension 0, may hold values from 0 to 23, as said below
- route_weights: int32 [512, 2], P(('groups', 'fsdp')), parts along dimension 0, may hold values from 1 to 65535, as said below
- w_gate: bfloat16 [8, 4096, 7168], P('expert', None, 'fsdp'), may hold values from -0.09375 to 0.09375
- w_up: bfloat16 [8, 4096, 7168], P('expert', None, 'fsdp'), may hold values from -0.09375 to 0.09375
- w_down: bfloat16 [8, 7168, 4096], P('expert', 'fsdp'), may hold values from -0.0625 to 0.0625
Outputs:
- layer_out: bfloat16 [512, 4096], P(('groups', 'fsdp'), 'expert'), parts along dimension 0
There are 2 independent parts, one for each index of `groups`. A program takes and returns all parts, laid end to end along the dimension named above; an argument that names none is the same for every part. Nothing has to cross between parts.
Inputs may be any that keep to these rules, and one draw needn't show every extreme that they name: `route_ids`: each row names two different experts. Among the rows of one block, no expert is named more than 24 times and no group of experts 2 g and 2 g + 1 more than 36 times; one expert, the same for all blocks, is named exactly 24 times in every block and its group exactly 36 times; every expert is named in every block. `route_slots`: within one block, the routes to one expert hold the slots 0 to their count - 1, each once. `route_weights`: the two entries of a row sum to 65536.
All inputs are finite; a program needn't handle non-finite values.
Results may differ from a plain program's by a relative error of at most 0.02.
Values may be sent and summed in bfloat16 or wider, within the bound.
No kernel may reach another device: no remote copies, remote signals or barrier semaphores. Data moves between devices by JAX's collectives and lax.ppermute only.
A program may use at most 192 MiB of HBM per device.

v0:
```python
import jax
import jax.numpy as jnp
from jax import lax
from jax.sharding import PartitionSpec as P

HEAD_DIM = 128
GCAP = 36
eps = 1e-05


def attend(queries, keys, values):
    block = queries.shape[0]
    context = keys.shape[1]
    kv_dev = keys.shape[2] // HEAD_DIM
    heads_dev = queries.shape[1] // HEAD_DIM
    group = heads_dev // kv_dev
    query_heads = queries.reshape(block, kv_dev, group, HEAD_DIM)
    key_heads = keys[0].reshape(context, kv_dev, HEAD_DIM)
    value_heads = values[0].reshape(context, kv_dev, HEAD_DIM)
    scores = jnp.einsum(
        "qcgd,kcd->cgqk", query_heads, key_heads, preferred_element_type=jnp.float32
    ) * HEAD_DIM ** (-0.5)
    key_pos = jnp.arange(context)
    query_pos = context - block + jnp.arange(block)
    allowed = key_pos[None, :] <= query_pos[:, None]
    masked = jnp.where(allowed, scores, -1e30)
    highest = jnp.max(masked, axis=-1, keepdims=True)
    weights = jnp.where(allowed, jnp.exp(masked - highest), 0.0)
    probs = (weights / jnp.sum(weights, axis=-1, keepdims=True)).astype(jnp.bfloat16)
    heads_out = jnp.einsum("cgqk,kcd->qcgd", probs, value_heads, preferred_element_type=jnp.float32)
    return heads_out.astype(jnp.bfloat16).reshape(block, heads_dev * HEAD_DIM)


def per_device(
    queries,
    keys,
    values,
    out_weight,
    residual,
    norm_gain,
    route_ids,
    route_slots,
    route_weights,
    w_gate,
    w_up,
    w_down,
):
    heads_out = attend(queries, keys, values)
    partial_attn = jnp.dot(
        heads_out,
        lax.all_gather(out_weight, "fsdp", axis=1, tiled=True),
        preferred_element_type=jnp.float32,
    )
    attn = lax.psum(partial_attn.astype(jnp.bfloat16), "expert").astype(jnp.float32)
    hstate = (residual.astype(jnp.float32) + attn).astype(jnp.bfloat16)
    state = hstate.astype(jnp.float32)
    scale = lax.rsqrt(jnp.mean(state * state, axis=-1, keepdims=True) + eps)
    normed = (state * scale * norm_gain).astype(jnp.bfloat16)
    group_index = lax.axis_index("expert")
    first_expert = 2 * group_index
    within = route_ids - first_expert
    in_group = (within >= 0) & (within < 2)
    lead_count = jnp.sum((route_ids == first_expert).astype(jnp.int32))
    target = jnp.where(in_group, route_slots + within * lead_count, -1)
    row_ids = jnp.arange(GCAP)
    one_hot = (
        (target[None, :, 0] == row_ids[:, None]) | (target[None, :, 1] == row_ids[:, None])
    ).astype(jnp.bfloat16)
    dispatch = jnp.dot(one_hot, normed, preferred_element_type=jnp.float32).astype(jnp.bfloat16)
    second = (row_ids >= lead_count).astype(jnp.bfloat16)
    rows = lax.all_gather(dispatch, "fsdp", axis=0, tiled=True)
    labels = lax.all_gather(second, "fsdp", axis=0, tiled=True)
    gate = jnp.einsum("nd,edf->enf", rows, w_gate, preferred_element_type=jnp.float32)
    upper = jnp.einsum("nd,edf->enf", rows, w_up, preferred_element_type=jnp.float32)
    labels_f = labels.astype(jnp.float32)
    keep = jnp.stack([1.0 - labels_f, labels_f], axis=0)[:, :, None]
    values_new = (jax.nn.silu(gate) * upper * keep).astype(jnp.bfloat16)
    flat_out = lax.psum_scatter(
        jnp.einsum("enf,efd->nd", values_new, w_down, preferred_element_type=jnp.float32).astype(
            jnp.bfloat16
        ),
        "fsdp",
        scatter_dimension=0,
        tiled=True,
    ).astype(jnp.float32)
    row_index = route_slots + within * lead_count
    safe_index = jnp.where(in_group, row_index, 0)
    shares = jnp.where(in_group, route_weights.astype(jnp.float32) / 65536.0, 0.0)
    picked = jnp.take(flat_out, safe_index, axis=0)
    contrib = jnp.sum(shares[:, :, None] * picked, axis=1)
    moe = lax.psum_scatter(
        contrib.astype(jnp.bfloat16), "expert", scatter_dimension=1, tiled=True
    ).astype(jnp.float32)
    width = moe.shape[1]
    own_state = lax.dynamic_slice_in_dim(hstate, group_index * width, width, 1)
    return (own_state.astype(jnp.float32) + moe).astype(jnp.bfloat16)


def solution(mesh):
    in_specs = (
        P(("groups", "fsdp"), "expert"),
        P(("groups", "fsdp"), None, "expert"),
        P(("groups", "fsdp"), None, "expert"),
        P("expert", "fsdp"),
        P(("groups", "fsdp"), None),
        P(),
        P(("groups", "fsdp"), None),
        P(("groups", "fsdp"), None),
        P(("groups", "fsdp"), None),
        P("expert", None, "fsdp"),
        P("expert", None, "fsdp"),
        P("expert", "fsdp", None),
    )
    out_specs = P(("groups", "fsdp"), "expert")
    return jax.shard_map(
        per_device, mesh=mesh, in_specs=in_specs, out_specs=out_specs, check_vma=False
    )
```

profile of v0, /device:TPU:0, one launch (start us, length us, event | category | flops | bytes accessed | tf_op | source)
XLA Modules:
  0.0 273.5 jit_solution(8926764271031604778)
XLA Ops:
  6.5 0.0 copy-start
  6.5 0.0 all-gather.4.cloned.1.call-start
  6.5 0.7 all-gather.4.cloned.1.call-update
  7.3 0.0 all-reduce.5.cloned.1.call-start
  7.3 0.1 iota_compare_fusion
  7.5 0.1 copy-done
  7.6 0.0 copy-start.8
  7.6 1.5 fusion.39
  9.1 0.5 fusion.13
  9.6 0.0 copy-done.8
  9.6 0.0 copy-start.4
  9.6 0.0 copy-start.7
  9.6 0.7 fusion.14
  10.3 0.1 copy.23
  10.4 0.0 copy-done.4
  10.4 0.6 fusion.35
  11.1 0.0 copy-done.7
  11.1 81.3 %all-gather.4.cloned.1.call-done = bf16[512,4096]{1,0:T(8,128)(2,1)} async-done(((bf16[512,1024]{1,0:T(8,128)(2,1)}), bf16[512,4096]{1,0:T(8,128)(2,1)}) %all-gather.4.cloned.1.call-update) | async-done | bytes 4194320 | tf_op jit(solution)/shard_map/all_gather | solution.py:51
  92.4 0.0 copy-start.5
  92.4 0.0 copy-start.3
  92.4 3.9 %convolution_convert_fusion = bf16[64,4096]{1,0:T(8,128)(2,1)} fusion(bf16[512,4096]{1,0:T(8,128)(2,1)} %all-gather.4.cloned.1.call-done, bf16[8,8,4,128]{3,2,1,0:T(4,128)(2,1)S(1)} %bitcast.74), kind=kOutput, calls=%fused_computation.3 | convolution fusion | flops 268697600 | bytes 4784128 | tf_op jit(solution)/shard_map/dot_general | solution.py:49
  96.3 0.0 copy-start.9
  96.3 0.0 copy-start.6
  96.3 0.0 all-reduce.5.cloned.1.call-update
  96.3 0.0 all-gather.6.cloned.1.call-start
  96.4 0.0 copy-done.5
  96.4 0.7 broadcast_select_fusion
  97.0 31.3 %all-reduce.5.cloned.1.call-done = bf16[64,4096]{1,0:T(8,128)(2,1)} async-done(((bf16[64,4096]{1,0:T(8,128)(2,1)}), bf16[64,4096]{1,0:T(8,128)(2,1)}) %all-reduce.5.cloned.1.call-update) | async-done | bytes 524304 | tf_op jit(solution)/shard_map/psum | solution.py:54
  128.4 0.0 copy-done.3
  128.4 1.3 fusion.15
  129.7 0.0 copy-start.2
  129.7 0.0 copy-done.9
  129.7 1.1 fusion.2
  130.8 0.0 all-gather.6.cloned.1.call-update
  130.8 0.0 reduce-scatter.4.cloned.1.call-start
  130.9 0.0 copy-done.6
  130.9 0.7 fusion.38
  132.2 0.7 compare_convert_fusion
  132.8 0.2 dynamic-update-slice
  133.1 11.8 %all-reduce = bf16[144]{0:T(256)(128)(2,1)S(1)} all-reduce(bf16[144]{0:T(256)(128)(2,1)S(1)} %dynamic-update-slice), channel_id=1, replica_groups=mesh['groups'=2,'fsdp'=4,'expert'=4] {'fsdp'}, use_global_device_ids=true, to_apply=%add | all-reduce | flops 144 | bytes 576
  144.9 0.7 compare_and_fusion
  145.5 0.1 copy.26
  145.6 0.1 reshape.63
  145.8 0.1 copy.25
  145.9 0.1 copy.24
  146.7 17.0 %all-gather.6.cloned.1.call-done = bf16[4,36,4096]{2,1,0:T(8,128)(2,1)} async-done(((bf16[1,36,4096]{2,1,0:T(8,128)(2,1)}), bf16[4,36,4096]{2,1,0:T(8,128)(2,1)}) %all-gather.6.cloned.1.call-update) | async-done | bytes 1179664 | tf_op jit(solution)/shard_map/all_gather | solution.py:71
  163.6 2.2 reshape.80
  165.9 12.0 %convolution_bitcast_fusion.2 = f32[2,144,1792]{2,1,0:T(8,128)S(1)} fusion(bf16[144,4096,1]{1,0,2:T(8,128)(2,1)} %reshape.80, bf16[2,4096,1792]{2,1,0:T(8,128)(2,1)} %param.21), kind=kOutput, calls=%fused_computation.7 | convolution fusion | flops 4227858432 | bytes 32604160 | tf_op jit(solution)/shard_map/nd,edf->enf/dot_general | solution.py:73
  177.9 0.0 copy-done.2
  177.9 22.2 %fusion.1 = bf16[144,4096]{1,0:T(8,128)(2,1)} fusion(bf16[2,1792,4096]{2,1,0:T(8,128)(2,1)} %param.23, bf16[144,4096,1]{1,0,2:T(8,128)(2,1)} %reshape.80, bf16[2,4096,1792]{2,1,0:T(8,128)(2,1)} %param.22, f32[2,144,1792]{2,1,0:T(8,128)S(1)} %convolution_bitcast_fusion.2, f32[2,144]{1,0:T(2,128)S(1)} %pad_maximum_fusion), kind=kOutput, calls=%fused_computation.2 | convolution fusion | flops 8459919360 | bytes 63145088 | tf_op jit(solution)/shard_map/enf,efd->nd/dot_general | solution.py:79
  200.1 29.1 %fusion = bf16[40,4096]{1,0:T(8,128)(2,1)S(1)} fusion(bf16[144,4096]{1,0:T(8,128)(2,1)} %fusion.1), kind=kCustom, calls=%all-reduce-scatter | all-reduce-scatter fusion | flops 655361 | bytes 1507840
  229.2 1.8 collective-permute-start
  231.0 2.3 collective-permute-done
  233.3 0.4 concatenate
  233.7 0.1 dynamic-slice_convert_fusion
  233.8 1.3 gather_fusion
  235.1 0.0 copy-start.1
  235.2 2.3 reshape.62
  237.4 6.0 %multiply_reduce_fusion = bf16[64,4096]{1,0:T(8,128)(2,1)} fusion(f32[64,2,4096]{2,1,0:T(2,128)} %reshape.62, pred[64,2]{1,0:T(8,128)(4,1)S(1)} %copy.25, f32[64,2]{1,0:T(8,128)S(1)} %copy.24), kind=kLoop, calls=%fused_computation.14 | loop fusion | flops 1310720 | bytes 2622080 | tf_op jit(solution)/shard_map/reduce_sum | solution.py:90
  243.5 0.0 reduce-scatter.4.cloned.1.call-update
  243.5 21.9 %reduce-scatter.4.cloned.1.call-done = bf16[64,1024]{1,0:T(8,128)(2,1)} async-done(((bf16[64,4096]{1,0:T(8,128)(2,1)}), bf16[64,1024]{1,0:T(8,128)(2,1)}) %reduce-scatter.4.cloned.1.call-update) | async-done | bytes 131088 | tf_op jit(solution)/shard_map/reduce_scatter | solution.py:91
  265.4 1.7 add_convert_fusion.1
  267.0 0.0 copy-done.1
  (10 shorter events, 0.1 us)
Async XLA Ops:
  6.5 1.0 copy-start
  6.5 85.9 %all-gather.4.cloned.1.call-start = ((), (), s32[]{:S(2)}) async-start(), calls=%async_computation.1 | async-start | bytes 5242880 | tf_op jit(solution)/shard_map/all_gather | solution.py:51
  7.3 121.1 %all-reduce.5.cloned.1.call-start = ((), (), s32[]{:S(2)}) async-start(), calls=%async_computation.2 | async-start | bytes 1048576 | tf_op jit(solution)/shard_map/psum | solution.py:54
  7.6 2.0 copy-start.8
  9.6 0.8 copy-start.4
  9.6 1.5 copy-start.7
  92.4 4.0 %copy-start.5 = (s32[64,2]{0,1:T(2,128)S(1)}, s32[64,2]{0,1:T(2,128)}, u32[]{:S(2)}) copy-start(s32[64,2]{0,1:T(2,128)} %param.19) | copy-start | bytes 1540
  92.4 36.0 %copy-start.3 = (bf16[64,4096]{1,0:T(8,128)(2,1)S(1)}, bf16[64,4096]{1,0:T(8,128)(2,1)}, u32[]{:S(2)}) copy-start(bf16[64,4096]{1,0:T(8,128)(2,1)} %param.16) | copy-start | bytes 1572868
  96.3 33.4 %copy-start.9 = (f32[4096]{0:T(1024)S(1)}, f32[4096]{0:T(1024)}, u32[]{:S(2)}) copy-start(f32[4096]{0:T(1024)} %param.17) | copy-start | bytes 49156
  96.3 34.6 %copy-start.6 = (u32[32]{0:T(128)S(1)}, u32[32]{0:T(128)}, u32[]{:S(2)}) copy-start(u32[32]{0:T(128)} %constant.60) | copy-start | bytes 388
  96.3 67.3 %all-gather.6.cloned.1.call-start = ((), (), s32[]{:S(2)}) async-start(), calls=%async_computation.4 | async-start | bytes 1638400 | tf_op jit(solution)/shard_map/all_gather | solution.py:71
  129.7 48.2 %copy-start.2 = (bf16[64,4096]{1,0:T(8,128)(2,1)}, bf16[64,4096]{1,0:T(8,128)(2,1)S(1)}, u32[]{:S(2)}) copy-start(bf16[64,4096]{1,0:T(8,128)(2,1)S(1)} %get-tuple-element.10) | copy-start | bytes 1572868
  130.8 134.5 %reduce-scatter.4.cloned.1.call-start = ((), (), s32[]{:S(2)}) async-start(), calls=%async_computation.3 | async-start | bytes 655360 | tf_op jit(solution)/shard_map/reduce_scatter | solution.py:91
  229.2 4.1 %collective-permute-start = (bf16[12,4096]{1,0:T(8,128)(2,1)S(1)}, bf16[12,4096]{1,0:T(8,128)(2,1)S(1)}, u32[]{:S(2)}, u32[]{:S(2)}) collective-permute-start(bf16[12,4096]{1,0:T(8,128)(2,1)S(1)} %slice.10), channel_id=1, source_target_pairs={{0,4},{4,8},{8,12},{1,5},{5,9},{9,13},{2,6},{6,10},{10,14},{3,7},{... | collective-permute-start | bytes 294920
  235.1 31.9 %copy-start.1 = (bf16[1,2048,128]{2,1,0:T(8,128)(2,1)S(1)}, bf16[1,2048,128]{2,1,0:T(8,128)(2,1)}, u32[]{:S(2)}) copy-start(bf16[1,2048,128]{2,1,0:T(8,128)(2,1)} %param.13) | copy-start | bytes 1572868
Sparse Core Ops, SparseCore 0:
  8.9 83.4 all-gather.3
  96.4 31.8 all-reduce.4
  130.9 32.6 all-gather.5
  243.6 21.6 reduce-scatter.3
where the time goes:
time: 274 us
  waiting for transfers between devices  155 us (57%)
  matrix products  41.3 us (15%)
  blocking collectives  40.8 us (15%)
  between operations  14.7 us (5%)
  other arithmetic  12.4 us (5%)
  local copies, waits for them, and re-layouts  7.87 us (3%)
    all_gather x1, waiting for transfers between devices, per_device(): lax.all_gather(out_weight, 'fsdp', axis=1, tiled=True)  81.3 us
    unnamed x2, blocking collectives  40.8 us
    psum x1, waiting for transfers between devices, per_device(): lax.psum(partial_attn.astype(jnp.bfloat16), 'expert').astype(jnp.float32)  31.3 us
    dot_general x1, matrix products, per_device(): jnp.einsum('enf,efd->nd', values_new, w_down, preferred_element_type=jnp....  22.2 us
    reduce_scatter x1, waiting for transfers between devices, per_device(): lax.psum_scatter(contrib.astype(jnp.bfloat16), 'expert', scatter_dimensio...  21.9 us
    all_gather x1, waiting for transfers between devices, per_device(): rows = lax.all_gather(dispatch, 'fsdp', axis=0, tiled=True)  17 us
    dot_general x1, matrix products, per_device(): jnp.einsum('nd,edf->enf', rows, w_gate, preferred_element_type=jnp.float32)  12 us
    reduce_sum x1, other arithmetic, per_device(): contrib = jnp.sum(shares[:, :, None] * picked, axis=1)  6.02 us
  transfers between devices with their start and end apart: 5, of which 5 were waited for; matrix products, arithmetic and copies ran while one was open for 3% of the time, Pallas kernels for 0%

commit v1 on v0

--- a/solution.py
+++ b/solution.py
@@ -51,7 +51,9 @@
         lax.all_gather(out_weight, "fsdp", axis=1, tiled=True),
         preferred_element_type=jnp.float32,
     )
-    attn = lax.psum(partial_attn.astype(jnp.bfloat16), "expert").astype(jnp.float32)
+    attn = jnp.sum(lax.all_gather(partial_attn.astype(jnp.bfloat16), "expert"), axis=0).astype(
+        jnp.float32
+    )
     hstate = (residual.astype(jnp.float32) + attn).astype(jnp.bfloat16)
     state = hstate.astype(jnp.float32)
     scale = lax.rsqrt(jnp.mean(state * state, axis=-1, keepdims=True) + eps)

time: 274 us -> 265 us (0.967)
  waiting for transfers between devices: 155 us -> 144 us
    psum x1 -> x0, waiting for transfers between devices: 31.3 us -> none  [per_device(): lax.psum(partial_attn.astype(jnp.bfloat16), 'expert').astype(jnp.float32)]
    all_gather x0 -> x1, waiting for transfers between devices: none -> 19.8 us  [per_device(): lax.all_gather(partial_attn.astype(jnp.bfloat16), 'expert')]
where the time goes in v1:
time: 265 us; the launch traced here: 264 us
  waiting for transfers between devices  144 us (54%)
  matrix products  41.3 us (16%)
  blocking collectives  40.9 us (15%)
  between operations  14.7 us (6%)
  other arithmetic  13.3 us (5%)
  local copies, waits for them, and re-layouts  8.66 us (3%)
    all_gather x1, waiting for transfers between devices, per_device(): lax.all_gather(out_weight, 'fsdp', axis=1, tiled=True)  82 us
    unnamed x2, blocking collectives  40.9 us
    dot_general x1, matrix products, per_device(): jnp.einsum('enf,efd->nd', values_new, w_down, preferred_element_type=jnp....  22.2 us
    reduce_scatter x1, waiting for transfers between devices, per_device(): lax.psum_scatter(contrib.astype(jnp.bfloat16), 'expert', scatter_dimensio...  21.9 us
    all_gather x1, waiting for transfers between devices, per_device(): lax.all_gather(partial_attn.astype(jnp.bfloat16), 'expert')  19.8 us
    all_gather x1, waiting for transfers between devices, per_device(): rows = lax.all_gather(dispatch, 'fsdp', axis=0, tiled=True)  16.9 us
    dot_general x1, matrix products, per_device(): jnp.einsum('nd,edf->enf', rows, w_gate, preferred_element_type=jnp.float32)  12 us
    reduce_sum x1, other arithmetic, per_device(): contrib = jnp.sum(shares[:, :, None] * picked, axis=1)  6.02 us
  transfers between devices with their start and end apart: 5, of which 5 were waited for; matrix products, arithmetic and copies ran while one was open for 3% of the time, Pallas kernels for 0%

profile of v1, /device:TPU:0, one launch (start us, length us, event | category | flops | bytes accessed | tf_op | source)
XLA Modules:
  0.0 264.3 jit_solution(15628697844452212698)
XLA Ops:
  6.5 0.0 copy-start
  6.5 0.0 all-gather.6.cloned.1.call-start
  6.5 0.7 all-gather.6.cloned.1.call-update
  7.3 0.0 all-gather.8.cloned.1.call-start
  7.3 0.1 iota_compare_fusion
  7.5 0.1 copy-done
  7.6 0.0 copy-start.8
  7.6 1.5 fusion.39
  9.1 0.5 fusion.13
  9.6 0.0 copy-done.8
  9.6 0.7 fusion.14
  10.3 0.1 copy.23
  10.4 82.0 %all-gather.6.cloned.1.call-done = bf16[512,4096]{1,0:T(8,128)(2,1)} async-done(((bf16[512,1024]{1,0:T(8,128)(2,1)}), bf16[512,4096]{1,0:T(8,128)(2,1)}) %all-gather.6.cloned.1.call-update) | async-done | bytes 4194320 | tf_op jit(solution)/shard_map/all_gather | solution.py:51
  92.4 0.0 copy-start.4
  92.4 0.0 copy-start.7
  92.4 0.0 copy-start.5
  92.4 3.9 %convolution_convert_fusion = bf16[64,4096]{1,0:T(8,128)(2,1)} fusion(bf16[512,4096]{1,0:T(8,128)(2,1)} %all-gather.6.cloned.1.call-done, bf16[8,8,4,128]{3,2,1,0:T(4,128)(2,1)S(1)} %bitcast.76), kind=kOutput, calls=%fused_computation.3 | convolution fusion | flops 268697600 | bytes 4784128 | tf_op jit(solution)/shard_map/dot_general | solution.py:49
  96.3 0.0 copy-start.3
  96.3 0.0 all-gather.8.cloned.1.call-update
  96.3 0.0 all-gather.10.cloned.1.call-start
  96.4 0.0 copy-done.4
  96.4 0.6 fusion.35
  97.0 0.0 copy-done.7
  97.0 0.0 copy-done.5
  97.0 0.7 broadcast_select_fusion
  97.7 19.8 %all-gather.8.cloned.1.call-done = bf16[256,4096]{1,0:T(8,128)(2,1)} async-done(((bf16[64,4096]{1,0:T(8,128)(2,1)}), bf16[256,4096]{1,0:T(8,128)(2,1)}) %all-gather.8.cloned.1.call-update) | async-done | bytes 2097168 | tf_op jit(solution)/shard_map/all_gather | solution.py:54
  117.5 0.0 copy-start.9
  117.5 2.0 reduce_sum.49
  119.5 0.0 copy-done.3
  119.5 0.0 copy-start.6
  119.5 0.3 fusion.15
  119.8 0.0 copy-start.2
  119.8 0.8 copy-done.2
  120.6 0.0 copy-done.9
  120.6 1.1 fusion.2
  121.7 0.0 all-gather.10.cloned.1.call-update
  121.7 0.0 reduce-scatter.4.cloned.1.call-start
  121.8 0.0 copy-done.6
  121.8 0.7 fusion.38
  123.1 0.7 compare_convert_fusion
  123.7 0.2 dynamic-update-slice
  124.0 11.8 %all-reduce = bf16[144]{0:T(256)(128)(2,1)S(1)} all-reduce(bf16[144]{0:T(256)(128)(2,1)S(1)} %dynamic-update-slice), channel_id=1, replica_groups=mesh['groups'=2,'fsdp'=4,'expert'=4] {'fsdp'}, use_global_device_ids=true, to_apply=%add | all-reduce | flops 144 | bytes 576
  135.8 0.7 compare_and_fusion
  136.4 0.1 copy.26
  136.5 0.1 reshape.63
  136.7 0.1 copy.25
  136.8 0.1 copy.24
  137.6 16.9 %all-gather.10.cloned.1.call-done = bf16[4,36,4096]{2,1,0:T(8,128)(2,1)} async-done(((bf16[1,36,4096]{2,1,0:T(8,128)(2,1)}), bf16[4,36,4096]{2,1,0:T(8,128)(2,1)}) %all-gather.10.cloned.1.call-update) | async-done | bytes 1179664 | tf_op jit(solution)/shard_map/all_gather | solution.py:73
  154.5 2.2 reshape.81
  156.8 12.0 %convolution_bitcast_fusion.2 = f32[2,144,1792]{2,1,0:T(8,128)S(1)} fusion(bf16[144,4096,1]{1,0,2:T(8,128)(2,1)} %reshape.81, bf16[2,4096,1792]{2,1,0:T(8,128)(2,1)} %param.21), kind=kOutput, calls=%fused_computation.7 | convolution fusion | flops 4227858432 | bytes 32604160 | tf_op jit(solution)/shard_map/nd,edf->enf/dot_general | solution.py:75
  168.8 22.2 %fusion.1 = bf16[144,4096]{1,0:T(8,128)(2,1)} fusion(bf16[2,1792,4096]{2,1,0:T(8,128)(2,1)} %param.23, bf16[144,4096,1]{1,0,2:T(8,128)(2,1)} %reshape.81, bf16[2,4096,1792]{2,1,0:T(8,128)(2,1)} %param.22, f32[2,144,1792]{2,1,0:T(8,128)S(1)} %convolution_bitcast_fusion.2, f32[2,144]{1,0:T(2,128)S(1)} %pad_maximum_fusion), kind=kOutput, calls=%fused_computation.2 | convolution fusion | flops 8459919360 | bytes 63145088 | tf_op jit(solution)/shard_map/enf,efd->nd/dot_general | solution.py:81
  190.9 29.1 %fusion = bf16[40,4096]{1,0:T(8,128)(2,1)S(1)} fusion(bf16[144,4096]{1,0:T(8,128)(2,1)} %fusion.1), kind=kCustom, calls=%all-reduce-scatter | all-reduce-scatter fusion | flops 655361 | bytes 1507840
  220.1 1.7 collective-permute-start
  221.8 2.3 collective-permute-done
  224.1 0.4 concatenate
  224.5 0.1 dynamic-slice_convert_fusion
  224.6 1.3 gather_fusion
  225.9 0.0 copy-start.1
  225.9 2.3 reshape.62
  228.2 6.0 %multiply_reduce_fusion = bf16[64,4096]{1,0:T(8,128)(2,1)} fusion(f32[64,2,4096]{2,1,0:T(2,128)} %reshape.62, pred[64,2]{1,0:T(8,128)(4,1)S(1)} %copy.25, f32[64,2]{1,0:T(8,128)S(1)} %copy.24), kind=kLoop, calls=%fused_computation.14 | loop fusion | flops 1310720 | bytes 2622080 | tf_op jit(solution)/shard_map/reduce_sum | solution.py:92
  234.2 0.0 reduce-scatter.4.cloned.1.call-update
  234.3 21.9 %reduce-scatter.4.cloned.1.call-done = bf16[64,1024]{1,0:T(8,128)(2,1)} async-done(((bf16[64,4096]{1,0:T(8,128)(2,1)}), bf16[64,1024]{1,0:T(8,128)(2,1)}) %reduce-scatter.4.cloned.1.call-update) | async-done | bytes 131088 | tf_op jit(solution)/shard_map/reduce_scatter | solution.py:93
  256.1 1.7 add_convert_fusion.1
  257.8 0.0 copy-done.1
  (10 shorter events, 0.1 us)
Async XLA Ops:
  6.5 1.0 copy-start
  6.5 85.9 %all-gather.6.cloned.1.call-start = ((), (), s32[]{:S(2)}) async-start(), calls=%async_computation.1 | async-start | bytes 5242880 | tf_op jit(solution)/shard_map/all_gather | solution.py:51
  7.3 110.2 %all-gather.8.cloned.1.call-start = ((), (), s32[]{:S(2)}) async-start(), calls=%async_computation.3 | async-start | bytes 2621440 | tf_op jit(solution)/shard_map/all_gather | solution.py:54
  7.6 2.0 copy-start.8
  92.4 4.0 %copy-start.4 = (s32[64,2]{0,1:T(2,128)S(1)}, s32[64,2]{0,1:T(2,128)}, u32[]{:S(2)}) copy-start(s32[64,2]{0,1:T(2,128)} %param.18) | copy-start | bytes 1540
  92.4 4.6 %copy-start.7 = (s32[64,2]{0,1:T(2,128)S(1)}, s32[64,2]{0,1:T(2,128)}, u32[]{:S(2)}) copy-start(s32[64,2]{0,1:T(2,128)} %param.20) | copy-start | bytes 1540
  92.4 4.6 %copy-start.5 = (s32[64,2]{0,1:T(2,128)S(1)}, s32[64,2]{0,1:T(2,128)}, u32[]{:S(2)}) copy-start(s32[64,2]{0,1:T(2,128)} %param.19) | copy-start | bytes 1540
  96.3 23.2 %copy-start.3 = (bf16[64,4096]{1,0:T(8,128)(2,1)S(1)}, bf16[64,4096]{1,0:T(8,128)(2,1)}, u32[]{:S(2)}) copy-start(bf16[64,4096]{1,0:T(8,128)(2,1)} %param.16) | copy-start | bytes 1572868
  96.3 58.2 %all-gather.10.cloned.1.call-start = ((), (), s32[]{:S(2)}) async-start(), calls=%async_computation.4 | async-start | bytes 1638400 | tf_op jit(solution)/shard_map/all_gather | solution.py:73
  117.5 3.1 %copy-start.9 = (f32[4096]{0:T(1024)S(1)}, f32[4096]{0:T(1024)}, u32[]{:S(2)}) copy-start(f32[4096]{0:T(1024)} %param.17) | copy-start | bytes 49156
  119.5 2.3 copy-start.6
  119.8 0.8 copy-start.2
  121.7 134.4 %reduce-scatter.4.cloned.1.call-start = ((), (), s32[]{:S(2)}) async-start(), calls=%async_computation.2 | async-start | bytes 655360 | tf_op jit(solution)/shard_map/reduce_scatter | solution.py:93
  220.1 4.0 %collective-permute-start = (bf16[12,4096]{1,0:T(8,128)(2,1)S(1)}, bf16[12,4096]{1,0:T(8,128)(2,1)S(1)}, u32[]{:S(2)}, u32[]{:S(2)}) collective-permute-start(bf16[12,4096]{1,0:T(8,128)(2,1)S(1)} %slice.10), channel_id=1, source_target_pairs={{0,4},{4,8},{8,12},{1,5},{5,9},{9,13},{2,6},{6,10},{10,14},{3,7},{... | collective-permute-start | bytes 294920
  225.9 31.9 %copy-start.1 = (bf16[1,2048,128]{2,1,0:T(8,128)(2,1)S(1)}, bf16[1,2048,128]{2,1,0:T(8,128)(2,1)}, u32[]{:S(2)}) copy-start(bf16[1,2048,128]{2,1,0:T(8,128)(2,1)} %param.13) | copy-start | bytes 1572868
Sparse Core Ops, SparseCore 0:
  8.9 83.4 all-gather.5
  96.4 21.0 all-gather.7
  121.8 32.6 all-gather.9
  234.4 21.6 reduce-scatter.3
